TPU v7x, 32 devices: a whole 2x2x4 slice. The times are simulated.
32 devices in a mesh: groups: 2 (over y), ctx: 4 (over z), role: 2 (over x), seq: 2 (over core).
Axes of the slice: x: 2, y: 2, z: 4, core: 2. Of those that a mesh axis runs over, the one named last changes fastest.
Arguments:
- queries: bfloat16 [32, 128, 576], P(('groups', 'role', 'seq'), 'ctx'), parts along dimension 0, may hold values from -24 to 24
- cache: bfloat16 [16, 4096, 576], P(('groups', 'role', 'seq'), 'ctx'), parts along dimension 0, may hold values from -4 to 4
- lengths: int32 [16], P(('groups', 'role', 'seq')), parts along dimension 0, may hold values from 4 to 4096, as said below
- positions: int32 [32], P(('groups', 'role', 'seq')), parts along dimension 0, may hold values from 0 to 4098, as said below
- value_up_weight: bfloat16 [128, 512, 128], P('ctx', ('role', 'seq')), may hold values from -0.25 to 0.25
- out_proj: bfloat16 [16384, 7168], P('ctx', ('role', 'seq')), may hold values from -0.046875 to 0.046875
- residual: bfloat16 [32, 7168], P('groups', ('role', 'seq')), parts along dimension 0, may hold values from -4 to 4
- norm_gain: float32 [7168], P(('role', 'seq')), may hold values from 0.5 to 1.5
- gate_weight: bfloat16 [7168, 9216], P(('role', 'seq'), 'ctx'), may hold values from -0.0625 to 0.0625
- up_weight: bfloat16 [7168, 9216], P(('role', 'seq'), 'ctx'), may hold values from -0.0625 to 0.0625
- down_weight: bfloat16 [9216, 7168], P('ctx', ('role', 'seq')), may hold values from -0.0625 to 0.0625
Outputs:
- layer_out: bfloat16 [32, 7168], P(('groups', 'ctx'), ('role', 'seq')), parts along dimension 0
There are 2 independent parts, one for each index of `groups`. A program takes and returns all parts, laid end to end along the dimension named above; an argument that names none is the same for every part. Nothing has to cross between parts.
Inputs may be any that keep to these rules, and one draw needn't show every extreme that they name: `lengths`: every sequence has at least 4 cached positions, and in every draw some sequence has all 4096. positions[r] lies between lengths[r // 2] - 4 and lengths[r // 2] + 2.
All inputs are finite; a program needn't handle non-finite values.
Results may differ from a plain program's by a relative error of at most 0.013.
Values may be sent and summed in bfloat16 or wider, within the bound.
A program may use at most 128 MiB of HBM per device.

v0:
```python
import jax
import jax.numpy as jnp
from jax import lax
from jax.sharding import PartitionSpec as P

D = 7168
HEADS = 128
LATENT = 512
ROPE = 64
VDIM = 128
MTP = 2
softmax_scale = 0.07216878364870323
epsilon = 1e-06


def settle_heads(pieces):
    maxima, totals, partial_value = pieces
    highest = jnp.max(maxima, axis=0)
    factor = jnp.exp(maxima - highest[None])
    denom = jnp.sum(factor * totals, axis=0)
    numer = jnp.sum(factor[..., None] * partial_value, axis=0)
    return (numer / denom[..., None]).astype(jnp.bfloat16)


def per_device(
    queries,
    cache,
    lengths,
    positions,
    value_up_weight,
    out_proj,
    residual,
    norm_gain,
    gate_weight,
    up_weight,
    down_weight,
):
    all_heads = lax.all_gather(queries, "ctx", axis=1, tiled=True)
    heads_here = queries.shape[1]
    width = LATENT + ROPE
    context_local = cache.shape[1]
    seq_here = cache.shape[0]
    offset = lax.axis_index("ctx") * context_local
    places = offset + jnp.arange(context_local, dtype=jnp.int32)
    maxima_list = []
    totals_list = []
    partial_list = []
    for number in range(seq_here):
        rows_pair = all_heads[MTP * number : MTP * (number + 1)].reshape(MTP * HEADS, width)
        keys_here = cache[number]
        limits = jnp.repeat(positions[MTP * number : MTP * (number + 1)], HEADS)
        length = lengths[number]

        def compute_block(rows_pair=rows_pair, keys_here=keys_here, limits=limits, length=length):
            scores = (
                jnp.dot(rows_pair, keys_here.T, preferred_element_type=jnp.float32) * softmax_scale
            )
            live = (places[None, :] < length) & (places[None, :] <= limits[:, None])
            block_max = jnp.max(jnp.where(live, scores, jnp.float32(-1e30)), axis=-1)
            probs = jnp.exp(
                jnp.where(live, scores - block_max[:, None], jnp.float32(-1e30))
            ).astype(jnp.bfloat16)
            block_weight_sum = jnp.sum(probs.astype(jnp.float32), axis=-1)
            block_out = jnp.dot(probs, keys_here[:, :LATENT], preferred_element_type=jnp.float32)
            return (block_max, block_weight_sum, block_out)

        block_max, block_weight_sum, block_out = compute_block()
        maxima_list.append(block_max.reshape(MTP, HEADS))
        totals_list.append(block_weight_sum.reshape(MTP, HEADS))
        partial_list.append(block_out.reshape(MTP, HEADS, LATENT))
    maxima = jnp.concatenate(maxima_list, axis=0)
    totals = jnp.concatenate(totals_list, axis=0)
    partial_value = jnp.concatenate(partial_list, axis=0)
    attended_values = settle_heads(
        (
            lax.all_to_all(maxima[None], "ctx", split_axis=2, concat_axis=0, tiled=True),
            lax.all_to_all(totals[None], "ctx", split_axis=2, concat_axis=0, tiled=True),
            lax.all_to_all(partial_value[None], "ctx", split_axis=2, concat_axis=0, tiled=True),
        )
    )
    mixed = jnp.einsum(
        "nut,utc->nuc",
        attended_values,
        lax.all_gather(value_up_weight, ("role", "seq"), axis=1, tiled=True),
        preferred_element_type=jnp.float32,
    )
    value_vectors = mixed.astype(jnp.bfloat16).reshape(attended_values.shape[0], heads_here * VDIM)
    per_head_terms = jnp.dot(
        lax.all_gather(value_vectors, ("role", "seq"), axis=0, tiled=True),
        out_proj,
        preferred_element_type=jnp.float32,
    )
    attn_out = lax.psum(per_head_terms, "ctx")
    resid = residual.astype(jnp.float32) + attn_out
    sumsq = lax.psum(jnp.sum(resid * resid, axis=1), ("role", "seq"))
    normed = (resid * lax.rsqrt(sumsq / D + epsilon)[:, None] * norm_gain[None, :]).astype(
        jnp.bfloat16
    )
    gate_term = jnp.dot(normed, gate_weight, preferred_element_type=jnp.float32)
    up_term = jnp.dot(normed, up_weight, preferred_element_type=jnp.float32)
    gate, up = lax.psum((gate_term, up_term), ("role", "seq"))
    hidden = (jax.nn.silu(gate) * up).astype(jnp.bfloat16)
    rows_here = resid.shape[0] // lax.axis_size("ctx")
    ffn_rows = lax.psum_scatter(
        jnp.dot(hidden, down_weight, preferred_element_type=jnp.float32),
        "ctx",
        scatter_dimension=0,
        tiled=True,
    )
    base_rows = lax.dynamic_slice_in_dim(resid, lax.axis_index("ctx") * rows_here, rows_here, 0)
    return (base_rows + ffn_rows).astype(jnp.bfloat16)


def solution(mesh):
    placed = (
        P(("groups", "role", "seq"), "ctx", None),
        P(("groups", "role", "seq"), "ctx", None),
        P(("groups", "role", "seq")),
        P(("groups", "role", "seq")),
        P("ctx", ("role", "seq"), None),
        P("ctx", ("role", "seq")),
        P("groups", ("role", "seq")),
        P(("role", "seq")),
        P(("role", "seq"), "ctx"),
        P(("role", "seq"), "ctx"),
        P("ctx", ("role", "seq")),
    )
    return jax.shard_map(
        per_device,
        mesh=mesh,
        in_specs=placed,
        out_specs=P(("groups", "ctx"), ("role", "seq")),
        check_vma=False,
    )
```

profile of v0, /device:TPU:0, one launch (start us, length us, event | category | flops | bytes accessed | tf_op | source)
XLA Modules:
  0.0 227.1 jit_solution(11326140525146923370)
XLA Ops:
  7.3 1.3 fusion.19
  8.6 1.3 fusion.12
  9.9 19.9 %all_gather.9 = bf16[4,128,576]{2,1,0:T(8,128)(2,1)S(1)} all-gather(bf16[4,32,576]{2,1,0:T(8,128)(2,1)} %param.11), channel_id=1, replica_groups=mesh['groups'=2,'ctx'=4,'role'=2,'seq'=2] {'ctx'}, dimensions={1}, use_global_device_ids=true | all-gather | bytes 737280 | tf_op jit(solution)/shard_map/all_gather | solution.py:38
  30.7 1.8 convolution_multiply_fusion
  32.6 0.9 select_reduce_fusion.1
  36.6 3.8 %all-to-all-start.2 = ((f32[4,1,128]{2,1,0:T(1,128)}), f32[4,1,128]{2,1,0:T(1,128)S(1)}, u32[]{:S(2)}, u32[]{:S(2)}) async-start(f32[4,1,128]{2,1,0:T(1,128)} %reshape.68), calls=%async_computation.2 | async-start | bytes 4096 | tf_op jit(solution)/shard_map/all_to_all | solution.py:77
  44.0 1.9 all-to-all-done.2
  45.9 3.2 %all-to-all-start = ((f32[4,1,128]{2,1,0:T(1,128)}), f32[4,1,128]{2,1,0:T(1,128)S(1)}, u32[]{:S(2)}, u32[]{:S(2)}) async-start(f32[4,1,128]{2,1,0:T(1,128)} %reshape.66), calls=%async_computation | async-start | bytes 4096 | tf_op jit(solution)/shard_map/all_to_all | solution.py:76
  49.1 1.4 maximum_bitcast_fusion
  50.6 4.1 %all-to-all-done = f32[4,1,128]{2,1,0:T(1,128)S(1)} async-done(((f32[4,1,128]{2,1,0:T(1,128)}), f32[4,1,128]{2,1,0:T(1,128)S(1)}, u32[]{:S(2)}, u32[]{:S(2)}) %all-to-all-start) | async-done | bytes 2080 | tf_op jit(solution)/shard_map/all_to_all | solution.py:76
  54.7 3.5 %all-to-all-start.1 = ((f32[1,4,128,512]{3,1,0,2:T(4,128)}), f32[1,4,128,512]{3,1,0,2:T(4,128)S(1)}, u32[]{:S(2)}, u32[]{:S(2)}) async-start(f32[1,4,128,512]{3,1,0,2:T(4,128)} %maximum_bitcast_fusion), calls=%async_computation.1 | async-start | bytes 2097152 | tf_op jit(solution)/shard_map/all_to_all | solution.py:78
  60.1 18.8 %all-to-all-done.1 = f32[1,4,128,512]{3,1,0,2:T(4,128)S(1)} async-done(((f32[1,4,128,512]{3,1,0,2:T(4,128)}), f32[1,4,128,512]{3,1,0,2:T(4,128)S(1)}, u32[]{:S(2)}, u32[]{:S(2)}) %all-to-all-start.1) | async-done | bytes 1048608 | tf_op jit(solution)/shard_map/all_to_all | solution.py:78
  79.4 2.8 %fusion = bf16[1,4,4096]{2,1,0:T(4,128)(2,1)S(1)} fusion(bf16[32,512,128]{2,1,0:T(8,128)(2,1)} %all-gather.3.cloned.1.call-done, bf16[4,32,512]{2,1,0:T(8,128)(2,1)S(1)} %divide_convert_fusion), kind=kOutput, calls=%fused_computation.5 | convolution fusion | flops 16793600 | bytes 4358144 | tf_op jit(solution)/shard_map/nut,utc->nuc/dot_general | solution.py:81
  82.2 5.4 %all-gather = bf16[4,4,4096]{2,1,0:T(4,128)(2,1)S(1)} all-gather(bf16[1,4,4096]{2,1,0:T(4,128)(2,1)S(1)} %fusion), channel_id=1, replica_groups=mesh['groups'=2,'ctx'=4,'role'=2,'seq'=2] {'role','seq'}, dimensions={0}, use_global_device_ids=true | all-gather | bytes 163840 | tf_op jit(solution)/shard_map/all_gather | solution.py:89
  87.7 7.8 %fusion.21 = f32[16,1792]{1,0:T(8,128)} fusion(bf16[16,4096]{1,0:T(8,128)(2,1)S(1)} %reshape.63, bf16[4096,1792]{1,0:T(8,128)(2,1)} %param.16), kind=kOutput, calls=%fused_computation.50 | convolution fusion | flops 234881024 | bytes 14925824 | tf_op jit(solution)/shard_map/dot_general | solution.py:88
  95.6 33.5 %all-reduce.6.cloned.1.call-done = f32[16,1792]{1,0:T(8,128)} async-done(((f32[16,1792]{1,0:T(8,128)}), f32[16,1792]{1,0:T(8,128)}) %all-reduce.6.cloned.1.call-update) | async-done | bytes 114704 | tf_op jit(solution)/shard_map/psum | solution.py:93
  129.1 1.0 multiply_reduce_fusion
  130.1 5.7 %psum.29 = f32[16]{0:T(128)S(1)} all-reduce(f32[16]{0:T(128)S(1)} %get-tuple-element.9), channel_id=1, replica_groups=mesh['groups'=2,'ctx'=4,'role'=2,'seq'=2] {'role','seq'}, use_global_device_ids=true, to_apply=%region_9.10 | all-reduce | flops 16 | bytes 128 | tf_op jit(solution)/shard_map/psum | solution.py:95
  135.8 5.2 %fusion.16 = f32[16,2304]{1,0:T(8,128)} fusion(bf16[1792,2304]{1,0:T(8,128)(2,1)} %param.19, f32[16,1792]{1,0:T(8,128)S(1)} %get-tuple-element.10, f32[1792]{0:T(1024)S(1)} %copy-done.1, f32[16]{0:T(128)S(1)} %add_rsqrt_fusion), kind=kOutput, calls=%fused_computation.46 | convolution fusion | flops 132206592 | bytes 8526912 | tf_op jit(solution)/shard_map/dot_general | solution.py:99
  141.1 5.3 %fusion.15 = f32[16,2304]{1,0:T(8,128)} fusion(bf16[1792,2304]{1,0:T(8,128)(2,1)} %param.20, f32[16,1792]{1,0:T(8,128)S(1)} %get-tuple-element.10, f32[1792]{0:T(1024)S(1)} %copy-done.1, f32[16]{0:T(128)S(1)} %add_rsqrt_fusion), kind=kOutput, calls=%fused_computation.45 | convolution fusion | flops 132206592 | bytes 8526912 | tf_op jit(solution)/shard_map/dot_general | solution.py:100
  146.4 32.9 %all-reduce.10.cloned.1.call-done = (f32[16,2304]{1,0:T(8,128)}, f32[16,2304]{1,0:T(8,128)}) async-done(((f32[16,2304]{1,0:T(8,128)}, f32[16,2304]{1,0:T(8,128)}), (f32[16,2304]{1,0:T(8,128)}, f32[16,2304]{1,0:T(8,128)})) %all-reduce.10.cloned.1.call-update) | async-done | bytes 294928 | tf_op jit(solution)/shard_map/psum | solution.py:101
  179.2 5.4 %fusion.7 = f32[16,1792]{1,0:T(8,128)} fusion(bf16[2304,1792]{1,0:T(8,128)(2,1)} %param.21, f32[16,2304]{1,0:T(8,128)} %get-tuple-element.7, f32[16,2304]{1,0:T(8,128)} %get-tuple-element.8), kind=kOutput, calls=%fused_computation.27 | convolution fusion | flops 132341760 | bytes 8667136 | tf_op jit(solution)/shard_map/dot_general | solution.py:105
  185.9 33.3 %all-reduce.8.cloned.1.call-done = f32[16,1792]{1,0:T(8,128)} async-done(((f32[16,1792]{1,0:T(8,128)}), f32[16,1792]{1,0:T(8,128)}) %all-reduce.8.cloned.1.call-update) | async-done | bytes 114704
  219.2 1.4 fusion.9
  (49 shorter events, 11.4 us)
Async XLA Ops:
  6.5 26.1 %copy-start = (bf16[2,1024,576]{1,2,0:T(8,128)(2,1)S(1)}, bf16[2,1024,576]{1,2,0:T(8,128)(2,1)}, u32[]{:S(2)}) copy-start(bf16[2,1024,576]{1,2,0:T(8,128)(2,1)} %param.12) | copy-start | bytes 7077892
  6.5 72.8 %all-gather.3.cloned.1.call-start = ((), (), s32[]{:S(2)}) async-start(), calls=%async_computation.3 | async-start | bytes 5242880 | tf_op jit(solution)/shard_map/all_gather | solution.py:84
  36.6 9.3 %all-to-all-start.2 = ((f32[4,1,128]{2,1,0:T(1,128)}), f32[4,1,128]{2,1,0:T(1,128)S(1)}, u32[]{:S(2)}, u32[]{:S(2)}) async-start(f32[4,1,128]{2,1,0:T(1,128)} %reshape.68), calls=%async_computation.2 | async-start | bytes 4096 | tf_op jit(solution)/shard_map/all_to_all | solution.py:77
  45.9 8.8 %all-to-all-start = ((f32[4,1,128]{2,1,0:T(1,128)}), f32[4,1,128]{2,1,0:T(1,128)S(1)}, u32[]{:S(2)}, u32[]{:S(2)}) async-start(f32[4,1,128]{2,1,0:T(1,128)} %reshape.66), calls=%async_computation | async-start | bytes 4096 | tf_op jit(solution)/shard_map/all_to_all | solution.py:76
  54.7 24.2 %all-to-all-start.1 = ((f32[1,4,128,512]{3,1,0,2:T(4,128)}), f32[1,4,128,512]{3,1,0,2:T(4,128)S(1)}, u32[]{:S(2)}, u32[]{:S(2)}) async-start(f32[1,4,128,512]{3,1,0,2:T(4,128)} %maximum_bitcast_fusion), calls=%async_computation.1 | async-start | bytes 2097152 | tf_op jit(solution)/shard_map/all_to_all | solution.py:78
  58.2 70.9 %all-reduce.6.cloned.1.call-start = ((), (), s32[]{:S(2)}) async-start(), calls=%async_computation.4 | async-start | bytes 229376 | tf_op jit(solution)/shard_map/psum | solution.py:93
  87.7 41.4 %copy-start.2 = (bf16[16,1792]{1,0:T(8,128)(2,1)S(1)}, bf16[16,1792]{1,0:T(8,128)(2,1)}, u32[]{:S(2)}) copy-start(bf16[16,1792]{1,0:T(8,128)(2,1)} %param.17) | copy-start | bytes 172036
  87.7 48.1 %copy-start.1 = (f32[1792]{0:T(1024)S(1)}, f32[1792]{0:T(1024)}, u32[]{:S(2)}) copy-start(f32[1792]{0:T(1024)} %param.18) | copy-start | bytes 21508
  95.6 83.7 %all-reduce.10.cloned.1.call-start = ((), (), s32[]{:S(2)}) async-start(), calls=%async_computation.6 | async-start | bytes 589824 | tf_op jit(solution)/shard_map/psum | solution.py:101
  146.3 72.8 %all-reduce.8.cloned.1.call-start = ((), (), s32[]{:S(2)}) async-start(), calls=%async_computation.5 | async-start | bytes 229376
  179.2 5.4 %copy-start.3 = (u32[32]{0:T(128)S(1)}, u32[32]{0:T(128)}, u32[]{:S(2)}) copy-start(u32[32]{0:T(128)} %constant.35) | copy-start | bytes 388
Sparse Core Ops, SparseCore 0:
  8.9 37.1 all-gather.2
  95.7 33.3 all-reduce.5
  146.4 32.7 all-reduce.9
  184.8 34.3 all-reduce.7
where the time goes:
time: 228 us; the launch traced here: 227 us
  waiting for transfers between devices  125 us (55%)
  blocking collectives  31 us (14%)
  matrix products  30.3 us (13%)
  between operations  14 us (6%)
  starting transfers between devices  10.7 us (5%)
  other arithmetic  9.47 us (4%)
  local copies, waits for them, and re-layouts  6.56 us (3%)
    unnamed x5, waiting for transfers between devices  34 us
    psum x1, waiting for transfers between devices, per_device(): attn_out = lax.psum(per_head_terms, 'ctx')  33.5 us
    psum x1, waiting for transfers between devices, per_device(): gate, up = lax.psum((gate_term, up_term), ('role', 'seq'))  32.9 us
    all_gather x1, blocking collectives, per_device(): all_heads = lax.all_gather(queries, 'ctx', axis=1, tiled=True)  19.9 us
    all_to_all x1, waiting for transfers between devices, per_device(): lax.all_to_all(partial_value[None], 'ctx', split_axis=2, concat_axis=0, t...  18.8 us
    dot_general x1, matrix products, per_device(): jnp.dot(lax.all_gather(value_vectors, ('role', 'seq'), axis=0, tiled=True...  7.84 us
    psum x1, blocking collectives, per_device(): sumsq = lax.psum(jnp.sum(resid * resid, axis=1), ('role', 'seq'))  5.66 us
    all_gather x1, blocking collectives, per_device(): lax.all_gather(value_vectors, ('role', 'seq'), axis=0, tiled=True)  5.41 us
  transfers between devices with their start and end apart: 7, of which 6 were waited for; matrix products, arithmetic and copies ran while one was open for 8% of the time, Pallas kernels for 0%

commit v1 on v0

--- a/solution.py
+++ b/solution.py
@@ -90,7 +90,7 @@
         out_proj,
         preferred_element_type=jnp.float32,
     )
-    attn_out = lax.psum(per_head_terms, "ctx")
+    attn_out = lax.all_gather(per_head_terms, "ctx").sum(axis=0)
     resid = residual.astype(jnp.float32) + attn_out
     sumsq = lax.psum(jnp.sum(resid * resid, axis=1), ("role", "seq"))
     normed = (resid * lax.rsqrt(sumsq / D + epsilon)[:, None] * norm_gain[None, :]).astype(

time: 228 us -> 207 us (0.908)
  waiting for transfers between devices: 125 us -> 90.3 us
  blocking collectives: 31 us -> 46.6 us
    psum x1 -> x0, waiting for transfers between devices: 33.5 us -> none  [per_device(): attn_out = lax.psum(per_head_terms, 'ctx')]
    all_gather x0 -> x1, blocking collectives: none -> 15.6 us  [per_device(): attn_out = lax.all_gather(per_head_terms, 'ctx').sum(axis=0)]
    unnamed x5 -> x4, waiting for transfers between devices: 34 us -> 34 us
  transfers between devices with their start and end apart: 7 -> 6, of which waited for: 6 -> 5; matrix products, arithmetic and copies ran while one was open for 8% -> 8% of each run, Pallas kernels for 0% -> 0%
where the time goes in v1:
time: 207 us; the launch traced here: 206 us
  waiting for transfers between devices  90.3 us (44%)
  blocking collectives  46.6 us (23%)
  matrix products  29.6 us (14%)
  between operations  14 us (7%)
  starting transfers between devices  10.6 us (5%)
  other arithmetic  8.61 us (4%)
  local copies, waits for them, and re-layouts  6.56 us (3%)
    unnamed x4, waiting for transfers between devices  34 us
    psum x1, waiting for transfers between devices, per_device(): gate, up = lax.psum((gate_term, up_term), ('role', 'seq'))  31.5 us
    all_gather x1, blocking collectives, per_device(): all_heads = lax.all_gather(queries, 'ctx', axis=1, tiled=True)  19.9 us
    all_to_all x1, waiting for transfers between devices, per_device(): lax.all_to_all(partial_value[None], 'ctx', split_axis=2, concat_axis=0, t...  18.8 us
    all_gather x1, blocking collectives, per_device(): attn_out = lax.all_gather(per_head_terms, 'ctx').sum(axis=0)  15.6 us
    dot_general x1, matrix products, per_device(): jnp.dot(lax.all_gather(value_vectors, ('role', 'seq'), axis=0, tiled=True...  7.19 us
    psum x1, blocking collectives, per_device(): sumsq = lax.psum(jnp.sum(resid * resid, axis=1), ('role', 'seq'))  5.66 us
    all_gather x1, blocking collectives, per_device(): lax.all_gather(value_vectors, ('role', 'seq'), axis=0, tiled=True)  5.41 us
  transfers between devices with their start and end apart: 6, of which 5 were waited for; matrix products, arithmetic and copies ran while one was open for 8% of the time, Pallas kernels for 0%

profile of v1, /device:TPU:0, one launch (start us, length us, event | category | flops | bytes accessed | tf_op | source)
XLA Modules:
  0.0 206.3 jit_solution(18373119654571800776)
XLA Ops:
  7.3 1.3 fusion.19
  8.6 1.3 fusion.12
  9.9 19.9 %all_gather.15 = bf16[4,128,576]{2,1,0:T(8,128)(2,1)S(1)} all-gather(bf16[4,32,576]{2,1,0:T(8,128)(2,1)} %param.11), channel_id=1, replica_groups=mesh['groups'=2,'ctx'=4,'role'=2,'seq'=2] {'ctx'}, dimensions={1}, use_global_device_ids=true | all-gather | bytes 737280 | tf_op jit(solution)/shard_map/all_gather | solution.py:38
  30.7 1.8 convolution_multiply_fusion
  32.6 0.9 select_reduce_fusion.1
  33.5 0.9 convert_reduce_fusion.1
  36.6 3.8 %all-to-all-start.2 = ((f32[4,1,128]{2,1,0:T(1,128)}), f32[4,1,128]{2,1,0:T(1,128)S(1)}, u32[]{:S(2)}, u32[]{:S(2)}) async-start(f32[4,1,128]{2,1,0:T(1,128)} %reshape.69), calls=%async_computation.2 | async-start | bytes 4096 | tf_op jit(solution)/shard_map/all_to_all | solution.py:77
  44.0 1.9 all-to-all-done.2
  45.9 3.2 %all-to-all-start = ((f32[4,1,128]{2,1,0:T(1,128)}), f32[4,1,128]{2,1,0:T(1,128)S(1)}, u32[]{:S(2)}, u32[]{:S(2)}) async-start(f32[4,1,128]{2,1,0:T(1,128)} %reshape.67), calls=%async_computation | async-start | bytes 4096 | tf_op jit(solution)/shard_map/all_to_all | solution.py:76
  49.1 1.4 maximum_bitcast_fusion
  50.6 4.1 %all-to-all-done = f32[4,1,128]{2,1,0:T(1,128)S(1)} async-done(((f32[4,1,128]{2,1,0:T(1,128)}), f32[4,1,128]{2,1,0:T(1,128)S(1)}, u32[]{:S(2)}, u32[]{:S(2)}) %all-to-all-start) | async-done | bytes 2080 | tf_op jit(solution)/shard_map/all_to_all | solution.py:76
  54.7 3.5 %all-to-all-start.1 = ((f32[1,4,128,512]{3,1,0,2:T(4,128)}), f32[1,4,128,512]{3,1,0,2:T(4,128)S(1)}, u32[]{:S(2)}, u32[]{:S(2)}) async-start(f32[1,4,128,512]{3,1,0,2:T(4,128)} %maximum_bitcast_fusion), calls=%async_computation.1 | async-start | bytes 2097152 | tf_op jit(solution)/shard_map/all_to_all | solution.py:78
  60.1 18.8 %all-to-all-done.1 = f32[1,4,128,512]{3,1,0,2:T(4,128)S(1)} async-done(((f32[1,4,128,512]{3,1,0,2:T(4,128)}), f32[1,4,128,512]{3,1,0,2:T(4,128)S(1)}, u32[]{:S(2)}, u32[]{:S(2)}) %all-to-all-start.1) | async-done | bytes 1048608 | tf_op jit(solution)/shard_map/all_to_all | solution.py:78
  79.4 2.8 %fusion = bf16[1,4,4096]{2,1,0:T(4,128)(2,1)S(1)} fusion(bf16[32,512,128]{2,1,0:T(8,128)(2,1)} %all-gather.4.cloned.1.call-done, bf16[4,32,512]{2,1,0:T(8,128)(2,1)S(1)} %divide_convert_fusion), kind=kOutput, calls=%fused_computation.5 | convolution fusion | flops 16793600 | bytes 4358144 | tf_op jit(solution)/shard_map/nut,utc->nuc/dot_general | solution.py:81
  82.2 5.4 %all-gather.1 = bf16[4,4,4096]{2,1,0:T(4,128)(2,1)S(1)} all-gather(bf16[1,4,4096]{2,1,0:T(4,128)(2,1)S(1)} %fusion), channel_id=1, replica_groups=mesh['groups'=2,'ctx'=4,'role'=2,'seq'=2] {'role','seq'}, dimensions={0}, use_global_device_ids=true | all-gather | bytes 163840 | tf_op jit(solution)/shard_map/all_gather | solution.py:89
  87.7 7.2 %fusion.21 = f32[16,1792]{1,0:T(8,128)S(1)} fusion(bf16[16,4096]{1,0:T(8,128)(2,1)S(1)} %reshape.64, bf16[4096,1792]{1,0:T(8,128)(2,1)} %param.16), kind=kOutput, calls=%fused_computation.50 | convolution fusion | flops 234881024 | bytes 14925824 | tf_op jit(solution)/shard_map/dot_general | solution.py:88
  94.9 15.6 %all-gather = f32[64,1792]{1,0:T(8,128)S(1)} all-gather(f32[16,1792]{1,0:T(8,128)S(1)} %fusion.21), channel_id=2, replica_groups=mesh['groups'=2,'ctx'=4,'role'=2,'seq'=2] {'ctx'}, dimensions={0}, use_global_device_ids=true | all-gather | bytes 573440 | tf_op jit(solution)/shard_map/all_gather | solution.py:93
  110.7 5.7 %psum.21 = f32[16]{0:T(128)S(1)} all-reduce(f32[16]{0:T(128)S(1)} %get-tuple-element.9), channel_id=1, replica_groups=mesh['groups'=2,'ctx'=4,'role'=2,'seq'=2] {'role','seq'}, use_global_device_ids=true, to_apply=%region_9.10 | all-reduce | flops 16 | bytes 128 | tf_op jit(solution)/shard_map/psum | solution.py:95
  116.4 5.2 %fusion.16 = f32[16,2304]{1,0:T(8,128)} fusion(bf16[1792,2304]{1,0:T(8,128)(2,1)} %param.19, f32[16,1792]{1,0:T(8,128)S(1)} %get-tuple-element.10, f32[1792]{0:T(1024)S(1)} %copy-done.1, f32[16]{0:T(128)S(1)} %add_rsqrt_fusion), kind=kOutput, calls=%fused_computation.46 | convolution fusion | flops 132206592 | bytes 8526912 | tf_op jit(solution)/shard_map/dot_general | solution.py:99
  121.6 5.3 %fusion.15 = f32[16,2304]{1,0:T(8,128)} fusion(bf16[1792,2304]{1,0:T(8,128)(2,1)} %param.20, f32[16,1792]{1,0:T(8,128)S(1)} %get-tuple-element.10, f32[1792]{0:T(1024)S(1)} %copy-done.1, f32[16]{0:T(128)S(1)} %add_rsqrt_fusion), kind=kOutput, calls=%fused_computation.45 | convolution fusion | flops 132206592 | bytes 8526912 | tf_op jit(solution)/shard_map/dot_general | solution.py:100
  127.0 31.5 %all-reduce.7.cloned.1.call-done = (f32[16,2304]{1,0:T(8,128)}, f32[16,2304]{1,0:T(8,128)}) async-done(((f32[16,2304]{1,0:T(8,128)}, f32[16,2304]{1,0:T(8,128)}), (f32[16,2304]{1,0:T(8,128)}, f32[16,2304]{1,0:T(8,128)})) %all-reduce.7.cloned.1.call-update) | async-done | bytes 294928 | tf_op jit(solution)/shard_map/psum | solution.py:101
  158.5 5.4 %fusion.7 = f32[16,1792]{1,0:T(8,128)} fusion(bf16[2304,1792]{1,0:T(8,128)(2,1)} %param.21, f32[16,2304]{1,0:T(8,128)} %get-tuple-element.7, f32[16,2304]{1,0:T(8,128)} %get-tuple-element.8), kind=kOutput, calls=%fused_computation.27 | convolution fusion | flops 132341760 | bytes 8667136 | tf_op jit(solution)/shard_map/dot_general | solution.py:105
  165.1 33.2 %all-reduce.5.cloned.1.call-done = f32[16,1792]{1,0:T(8,128)} async-done(((f32[16,1792]{1,0:T(8,128)}), f32[16,1792]{1,0:T(8,128)}) %all-reduce.5.cloned.1.call-update) | async-done | bytes 114704
  198.3 1.4 fusion.9
  (48 shorter events, 10.6 us)
Async XLA Ops:
  6.5 26.1 %copy-start = (bf16[2,1024,576]{1,2,0:T(8,128)(2,1)S(1)}, bf16[2,1024,576]{1,2,0:T(8,128)(2,1)}, u32[]{:S(2)}) copy-start(bf16[2,1024,576]{1,2,0:T(8,128)(2,1)} %param.12) | copy-start | bytes 7077892
  6.5 72.8 %all-gather.4.cloned.1.call-start = ((), (), s32[]{:S(2)}) async-start(), calls=%async_computation.3 | async-start | bytes 5242880 | tf_op jit(solution)/shard_map/all_gather | solution.py:84
  36.6 9.3 %all-to-all-start.2 = ((f32[4,1,128]{2,1,0:T(1,128)}), f32[4,1,128]{2,1,0:T(1,128)S(1)}, u32[]{:S(2)}, u32[]{:S(2)}) async-start(f32[4,1,128]{2,1,0:T(1,128)} %reshape.69), calls=%async_computation.2 | async-start | bytes 4096 | tf_op jit(solution)/shard_map/all_to_all | solution.py:77
  45.9 8.8 %all-to-all-start = ((f32[4,1,128]{2,1,0:T(1,128)}), f32[4,1,128]{2,1,0:T(1,128)S(1)}, u32[]{:S(2)}, u32[]{:S(2)}) async-start(f32[4,1,128]{2,1,0:T(1,128)} %reshape.67), calls=%async_computation | async-start | bytes 4096 | tf_op jit(solution)/shard_map/all_to_all | solution.py:76
  54.7 24.2 %all-to-all-start.1 = ((f32[1,4,128,512]{3,1,0,2:T(4,128)}), f32[1,4,128,512]{3,1,0,2:T(4,128)S(1)}, u32[]{:S(2)}, u32[]{:S(2)}) async-start(f32[1,4,128,512]{3,1,0,2:T(4,128)} %maximum_bitcast_fusion), calls=%async_computation.1 | async-start | bytes 2097152 | tf_op jit(solution)/shard_map/all_to_all | solution.py:78
  58.2 100.2 %all-reduce.7.cloned.1.call-start = ((), (), s32[]{:S(2)}) async-start(), calls=%async_computation.5 | async-start | bytes 589824 | tf_op jit(solution)/shard_map/psum | solution.py:101
  87.7 22.9 %copy-start.2 = (bf16[16,1792]{1,0:T(8,128)(2,1)S(1)}, bf16[16,1792]{1,0:T(8,128)(2,1)}, u32[]{:S(2)}) copy-start(bf16[16,1792]{1,0:T(8,128)(2,1)} %param.17) | copy-start | bytes 172036
  87.7 28.7 %copy-start.1 = (f32[1792]{0:T(1024)S(1)}, f32[1792]{0:T(1024)}, u32[]{:S(2)}) copy-start(f32[1792]{0:T(1024)} %param.18) | copy-start | bytes 21508
  126.9 71.4 %all-reduce.5.cloned.1.call-start = ((), (), s32[]{:S(2)}) async-start(), calls=%async_computation.4 | async-start | bytes 229376
  158.5 5.4 %copy-start.3 = (u32[32]{0:T(128)S(1)}, u32[32]{0:T(128)}, u32[]{:S(2)}) copy-start(u32[32]{0:T(128)} %constant.35) | copy-start | bytes 388
Sparse Core Ops, SparseCore 0:
  8.9 37.1 all-gather.3
  127.0 31.3 all-reduce.6
  164.0 34.3 all-reduce.4
